TPU v7x, 32 devices: a whole 2x2x4 slice. The times are simulated.
32 devices in a mesh: groups: 2 (over x), seq: 16 (over z, y, core).
Axes of the slice: x: 2, y: 2, z: 4, core: 2. Of those that a mesh axis runs over, the one named last changes fastest.
Arguments:
- queries: bfloat16 [1024, 2048], P(('groups', 'seq')), parts along dimension 0, may hold values from -132 to 132
- fresh_keys: bfloat16 [1024, 2048], P(('groups', 'seq')), parts along dimension 0, may hold values from -6 to 6
- fresh_values: bfloat16 [1024, 2048], P(('groups', 'seq')), parts along dimension 0, may hold values from -48 to 48
- stale_keys: bfloat16 [1024, 2048], P(('groups', 'seq')), parts along dimension 0, may hold values from -6 to 6
- stale_values: bfloat16 [1024, 2048], P(('groups', 'seq')), parts along dimension 0, may hold values from -48 to 48
- patch_sizes: int32 [8], P('groups'), parts along dimension 0, may hold values from 1 to 256, 512 in all
Outputs:
- attended: bfloat16 [1024, 2048], P(('groups', 'seq')), parts along dimension 0
There are 2 independent parts, one for each index of `groups`. A program takes and returns all parts, laid end to end along the dimension named above; each array names one. Nothing has to cross between parts.
Inputs may be any that keep to these rules, and one draw needn't show every extreme that they name: `patch_sizes`: the patch lengths sum to 512.
All inputs are finite; a program needn't handle non-finite values.
Results may differ from a plain program's by a relative error of at most 0.006.
Values may be sent and summed in bfloat16 or wider, within the bound.
No kernel may reach another device: no remote copies, remote signals or barrier semaphores. Data moves between devices by JAX's collectives and lax.ppermute only.
A program may use at most 64 MiB of HBM per device.

v0:
```python
import jax
import jax.numpy as jnp
from jax import lax
from jax.sharding import PartitionSpec as P

H = 16


def shifted(block, axis, distance):
    devices = range(lax.axis_size(axis))
    route = [((i - distance) % len(devices), i) for i in devices]
    return lax.ppermute(block, axis, route)


def shards(queries, fresh_keys, fresh_values, stale_keys, stale_values, patch_sizes):
    local_rows, columns = queries.shape
    head_size = columns // H
    devices = lax.axis_size("seq")
    query_groups = devices // H
    sub_rows = local_rows // query_groups
    shape_in = (sub_rows, devices, head_size)
    moved = (
        lax.all_to_all(queries.reshape(shape_in), "seq", split_axis=1, concat_axis=0, tiled=True),
        lax.all_to_all(
            fresh_keys.reshape(shape_in), "seq", split_axis=1, concat_axis=0, tiled=True
        ),
        lax.all_to_all(
            fresh_values.reshape(shape_in), "seq", split_axis=1, concat_axis=0, tiled=True
        ),
        lax.all_to_all(
            stale_keys.reshape(shape_in), "seq", split_axis=1, concat_axis=0, tiled=True
        ),
        lax.all_to_all(
            stale_values.reshape(shape_in), "seq", split_axis=1, concat_axis=0, tiled=True
        ),
    )
    query_rows = moved[0].reshape(-1, head_size)
    stacked = jnp.stack(
        [
            moved[1].reshape(-1, head_size),
            moved[2].reshape(-1, head_size),
            moved[3].reshape(-1, head_size),
            moved[4].reshape(-1, head_size),
        ]
    )
    own_group = lax.axis_index("seq") // H
    patch_ends = jnp.cumsum(patch_sizes)[:-1]
    positions = (
        jnp.arange(devices, dtype=jnp.int32)[:, None] * local_rows
        + jnp.arange(sub_rows, dtype=jnp.int32)[None, :] * query_groups
    ).reshape(-1)

    def patch_of(group):
        hits = positions[:, None] + group >= patch_ends[None, :]
        return jnp.sum(hits.astype(jnp.int32), axis=1)

    score_scale = head_size ** (-0.5)
    contract = (((1,), (1,)), ((), ()))
    query_patch = patch_of(own_group)

    def absorb(carry_state, key_block, source_group):
        running_max, denominator, numerator = carry_state
        is_fresh = patch_of(source_group)[None, :] <= query_patch[:, None]
        fresh_scores = lax.dot_general(
            query_rows, key_block[0], contract, preferred_element_type=jnp.float32
        )
        stale_scores = lax.dot_general(
            query_rows, key_block[2], contract, preferred_element_type=jnp.float32
        )
        scores = jnp.where(is_fresh, fresh_scores, stale_scores) * score_scale
        new_max = jnp.maximum(running_max, jnp.max(scores, axis=1, keepdims=True))
        rescale = jnp.exp(running_max - new_max)
        weights = jnp.exp(scores - new_max)
        denominator = denominator * rescale + jnp.sum(weights, axis=1, keepdims=True)
        rounded = weights.astype(jnp.bfloat16)
        zeroes = jnp.zeros_like(rounded)
        numerator = numerator * rescale + jnp.dot(
            jnp.where(is_fresh, rounded, zeroes), key_block[1], preferred_element_type=jnp.float32
        )
        numerator = numerator + jnp.dot(
            jnp.where(is_fresh, zeroes, rounded), key_block[3], preferred_element_type=jnp.float32
        )
        return (new_max, denominator, numerator)

    query_count = query_rows.shape[0]
    carry_state = (
        jnp.full((query_count, 1), -1e30, jnp.float32),
        jnp.zeros((query_count, 1), jnp.float32),
        jnp.zeros((query_count, head_size), jnp.float32),
    )
    carry_state = absorb(carry_state, stacked, own_group)
    travelling = stacked
    for offset in range(1, query_groups):
        travelling = shifted(travelling, "seq", H)
        carry_state = absorb(carry_state, travelling, (own_group - offset) % query_groups)
    attended = (carry_state[2] / carry_state[1]).astype(jnp.bfloat16)
    returned = lax.all_to_all(
        attended.reshape(devices, sub_rows, 1, head_size),
        "seq",
        split_axis=0,
        concat_axis=2,
        tiled=True,
    )
    return returned.reshape(local_rows, columns)


def solution(mesh):
    in_specs = (
        P(("groups", "seq"), None),
        P(("groups", "seq"), None),
        P(("groups", "seq"), None),
        P(("groups", "seq"), None),
        P(("groups", "seq"), None),
        P("groups"),
    )
    out_specs = P(("groups", "seq"), None)
    return jax.shard_map(shards, mesh=mesh, in_specs=in_specs, out_specs=out_specs, check_vma=False)
```

profile of v0, /device:TPU:0, one launch (start us, length us, event | category | flops | bytes accessed | tf_op | source)
XLA Modules:
  0.0 74.3 jit_solution(5553754712294257362)
XLA Ops:
  0.0 0.9 %copy-done = bf16[32,2048]{1,0:T(8,128)(2,1)S(1)} copy-done((bf16[32,2048]{1,0:T(8,128)(2,1)S(1)}, bf16[32,2048]{1,0:T(8,128)(2,1)}, u32[]{:S(2)}) %copy-start) | copy-done | bytes 131096
  0.9 0.7 copy_bitcast_fusion.5
  1.6 7.5 %all-to-all-start = ((bf16[32,16,128]{2,0,1:T(8,128)(2,1)}), bf16[32,16,128]{2,0,1:T(8,128)(2,1)S(1)}, u32[]{:S(2)}, u32[]{:S(2)}) async-start(bf16[32,16,128]{2,0,1:T(8,128)(2,1)} %copy_bitcast_fusion.5), calls=%async_computation | async-start | bytes 262144 | tf_op jit(solution)/shard_map/all_to_all | solution.py:23
  9.2 0.6 copy-done.5
  10.0 0.7 copy_bitcast_fusion.4
  10.7 0.3 copy-done.2
  10.9 0.7 copy_bitcast_fusion.3
  11.9 0.7 copy_bitcast_fusion.2
  12.6 4.5 %all-to-all-done = bf16[32,16,128]{2,0,1:T(8,128)(2,1)S(1)} async-done(((bf16[32,16,128]{2,0,1:T(8,128)(2,1)}), bf16[32,16,128]{2,0,1:T(8,128)(2,1)S(1)}, u32[]{:S(2)}, u32[]{:S(2)}) %all-to-all-start) | async-done | bytes 131104 | tf_op jit(solution)/shard_map/all_to_all | solution.py:23
  17.0 3.5 %all-to-all-start.1 = ((bf16[32,16,128]{2,0,1:T(8,128)(2,1)}), bf16[32,16,128]{2,0,1:T(8,128)(2,1)S(1)}, u32[]{:S(2)}, u32[]{:S(2)}) async-start(bf16[32,16,128]{2,0,1:T(8,128)(2,1)} %copy_bitcast_fusion.4), calls=%async_computation.1 | async-start | bytes 262144 | tf_op jit(solution)/shard_map/all_to_all | solution.py:24
  20.6 0.7 copy_bitcast_fusion.1
  21.3 7.1 %all-to-all-done.1 = bf16[32,16,128]{2,0,1:T(8,128)(2,1)S(1)} async-done(((bf16[32,16,128]{2,0,1:T(8,128)(2,1)}), bf16[32,16,128]{2,0,1:T(8,128)(2,1)S(1)}, u32[]{:S(2)}, u32[]{:S(2)}) %all-to-all-start.1) | async-done | bytes 131104 | tf_op jit(solution)/shard_map/all_to_all | solution.py:24
  28.4 3.5 %all-to-all-start.2 = ((bf16[32,16,128]{2,0,1:T(8,128)(2,1)}), bf16[32,16,128]{2,0,1:T(8,128)(2,1)S(1)}, u32[]{:S(2)}, u32[]{:S(2)}) async-start(bf16[32,16,128]{2,0,1:T(8,128)(2,1)} %copy_bitcast_fusion.3), calls=%async_computation.2 | async-start | bytes 262144 | tf_op jit(solution)/shard_map/all_to_all | solution.py:30
  31.9 0.3 fusion.17
  32.2 7.6 %all-to-all-done.2 = bf16[32,16,128]{2,0,1:T(8,128)(2,1)S(1)} async-done(((bf16[32,16,128]{2,0,1:T(8,128)(2,1)}), bf16[32,16,128]{2,0,1:T(8,128)(2,1)S(1)}, u32[]{:S(2)}, u32[]{:S(2)}) %all-to-all-start.2) | async-done | bytes 131104 | tf_op jit(solution)/shard_map/all_to_all | solution.py:30
  39.8 3.5 %all-to-all-start.3 = ((bf16[32,16,128]{2,0,1:T(8,128)(2,1)}), bf16[32,16,128]{2,0,1:T(8,128)(2,1)S(1)}, u32[]{:S(2)}, u32[]{:S(2)}) async-start(bf16[32,16,128]{2,0,1:T(8,128)(2,1)} %copy_bitcast_fusion.2), calls=%async_computation.3 | async-start | bytes 262144 | tf_op jit(solution)/shard_map/all_to_all | solution.py:27
  43.3 0.3 fusion.16
  43.9 7.3 %all-to-all-done.3 = bf16[32,16,128]{2,0,1:T(8,128)(2,1)S(1)} async-done(((bf16[32,16,128]{2,0,1:T(8,128)(2,1)}), bf16[32,16,128]{2,0,1:T(8,128)(2,1)S(1)}, u32[]{:S(2)}, u32[]{:S(2)}) %all-to-all-start.3) | async-done | bytes 131104 | tf_op jit(solution)/shard_map/all_to_all | solution.py:27
  51.2 3.5 %all-to-all-start.4 = ((bf16[32,16,128]{2,0,1:T(8,128)(2,1)}), bf16[32,16,128]{2,0,1:T(8,128)(2,1)S(1)}, u32[]{:S(2)}, u32[]{:S(2)}) async-start(bf16[32,16,128]{2,0,1:T(8,128)(2,1)} %copy_bitcast_fusion.1), calls=%async_computation.4 | async-start | bytes 262144 | tf_op jit(solution)/shard_map/all_to_all | solution.py:33
  54.7 0.4 convolution_add_fusion.1
  55.2 7.4 %all-to-all-done.4 = bf16[32,16,128]{2,0,1:T(8,128)(2,1)S(1)} async-done(((bf16[32,16,128]{2,0,1:T(8,128)(2,1)}), bf16[32,16,128]{2,0,1:T(8,128)(2,1)S(1)}, u32[]{:S(2)}, u32[]{:S(2)}) %all-to-all-start.4) | async-done | bytes 131104 | tf_op jit(solution)/shard_map/all_to_all | solution.py:33
  62.6 0.5 fusion.2
  63.1 10.5 %all_to_all.90 = bf16[16,32,1,128]{3,1,2,0:T(8,128)(2,1)S(1)} all-to-all(bf16[16,32,1,128]{3,1,2,0:T(8,128)(2,1)S(1)} %bitcast.79), channel_id=1, replica_groups=mesh['groups'=2,'seq'=16] {'seq'}, dimensions={0} | all-to-all | bytes 262144 | tf_op jit(solution)/shard_map/all_to_all | solution.py:97
  73.6 0.7 copy.47
  (19 shorter events, 0.8 us)
Async XLA Ops:
  0.0 0.9 %copy-start = (bf16[32,2048]{1,0:T(8,128)(2,1)S(1)}, bf16[32,2048]{1,0:T(8,128)(2,1)}, u32[]{:S(2)}) copy-start(bf16[32,2048]{1,0:T(8,128)(2,1)} %param.6) | copy-start | bytes 393220
  1.6 8.4 %copy-start.1 = (bf16[32,2048]{1,0:T(8,128)(2,1)S(1)}, bf16[32,2048]{1,0:T(8,128)(2,1)}, u32[]{:S(2)}) copy-start(bf16[32,2048]{1,0:T(8,128)(2,1)} %param.7) | copy-start | bytes 393220
  1.6 15.5 %all-to-all-start = ((bf16[32,16,128]{2,0,1:T(8,128)(2,1)}), bf16[32,16,128]{2,0,1:T(8,128)(2,1)S(1)}, u32[]{:S(2)}, u32[]{:S(2)}) async-start(bf16[32,16,128]{2,0,1:T(8,128)(2,1)} %copy_bitcast_fusion.5), calls=%async_computation | async-start | bytes 262144 | tf_op jit(solution)/shard_map/all_to_all | solution.py:23
  9.2 0.7 copy-start.5
  10.0 1.0 %copy-start.2 = (bf16[32,2048]{1,0:T(8,128)(2,1)S(1)}, bf16[32,2048]{1,0:T(8,128)(2,1)}, u32[]{:S(2)}) copy-start(bf16[32,2048]{1,0:T(8,128)(2,1)} %param.9) | copy-start | bytes 393220
  10.9 1.0 %copy-start.3 = (bf16[32,2048]{1,0:T(8,128)(2,1)S(1)}, bf16[32,2048]{1,0:T(8,128)(2,1)}, u32[]{:S(2)}) copy-start(bf16[32,2048]{1,0:T(8,128)(2,1)} %param.8) | copy-start | bytes 393220
  12.6 8.1 %copy-start.4 = (bf16[32,2048]{1,0:T(8,128)(2,1)S(1)}, bf16[32,2048]{1,0:T(8,128)(2,1)}, u32[]{:S(2)}) copy-start(bf16[32,2048]{1,0:T(8,128)(2,1)} %param.10) | copy-start | bytes 393220
  17.0 11.4 %all-to-all-start.1 = ((bf16[32,16,128]{2,0,1:T(8,128)(2,1)}), bf16[32,16,128]{2,0,1:T(8,128)(2,1)S(1)}, u32[]{:S(2)}, u32[]{:S(2)}) async-start(bf16[32,16,128]{2,0,1:T(8,128)(2,1)} %copy_bitcast_fusion.4), calls=%async_computation.1 | async-start | bytes 262144 | tf_op jit(solution)/shard_map/all_to_all | solution.py:24
  28.4 11.4 %all-to-all-start.2 = ((bf16[32,16,128]{2,0,1:T(8,128)(2,1)}), bf16[32,16,128]{2,0,1:T(8,128)(2,1)S(1)}, u32[]{:S(2)}, u32[]{:S(2)}) async-start(bf16[32,16,128]{2,0,1:T(8,128)(2,1)} %copy_bitcast_fusion.3), calls=%async_computation.2 | async-start | bytes 262144 | tf_op jit(solution)/shard_map/all_to_all | solution.py:30
  39.8 11.4 %all-to-all-start.3 = ((bf16[32,16,128]{2,0,1:T(8,128)(2,1)}), bf16[32,16,128]{2,0,1:T(8,128)(2,1)S(1)}, u32[]{:S(2)}, u32[]{:S(2)}) async-start(bf16[32,16,128]{2,0,1:T(8,128)(2,1)} %copy_bitcast_fusion.2), calls=%async_computation.3 | async-start | bytes 262144 | tf_op jit(solution)/shard_map/all_to_all | solution.py:27
  51.2 11.4 %all-to-all-start.4 = ((bf16[32,16,128]{2,0,1:T(8,128)(2,1)}), bf16[32,16,128]{2,0,1:T(8,128)(2,1)S(1)}, u32[]{:S(2)}, u32[]{:S(2)}) async-start(bf16[32,16,128]{2,0,1:T(8,128)(2,1)} %copy_bitcast_fusion.1), calls=%async_computation.4 | async-start | bytes 262144 | tf_op jit(solution)/shard_map/all_to_all | solution.py:33
where the time goes:
time: 74.9 us; the launch traced here: 74.3 us
  waiting for transfers between devices  33.9 us (45%)
  starting transfers between devices  21.6 us (29%)
  blocking collectives  10.5 us (14%)
  local copies, waits for them, and re-layouts  6.15 us (8%)
  matrix products  1.53 us (2%)
    all_to_all x1, blocking collectives, shards(): lax.all_to_all(attended.reshape(devices, sub_rows, 1, head_size), 'seq',...  10.5 us
    all_to_all x1, waiting for transfers between devices, shards(): lax.all_to_all(stale_keys.reshape(shape_in), 'seq', split_axis=1, concat_...  7.57 us
    all_to_all x1, starting transfers between devices, shards(): lax.all_to_all(queries.reshape(shape_in), 'seq', split_axis=1, concat_axi...  7.55 us
    all_to_all x1, waiting for transfers between devices, shards(): lax.all_to_all(stale_values.reshape(shape_in), 'seq', split_axis=1, conca...  7.43 us
    all_to_all x1, waiting for transfers between devices, shards(): lax.all_to_all(fresh_values.reshape(shape_in), 'seq', split_axis=1, conca...  7.33 us
    all_to_all x1, waiting for transfers between devices, shards(): lax.all_to_all(fresh_keys.reshape(shape_in), 'seq', split_axis=1, concat_...  7.11 us
    all_to_all x1, waiting for transfers between devices, shards(): lax.all_to_all(queries.reshape(shape_in), 'seq', split_axis=1, concat_axi...  4.46 us
    all_to_all x1, starting transfers between devices, shards(): lax.all_to_all(fresh_values.reshape(shape_in), 'seq', split_axis=1, conca...  3.51 us
  transfers between devices with their start and end apart: 5, of which 5 were waited for; matrix products, arithmetic and copies ran while one was open for 6% of the time, Pallas kernels for 0%

commit v1 on v0

v1 whole, which is shorter than its diff:
```python
import functools
import math

import jax
import jax.numpy as jnp
from jax import lax
from jax.experimental import pallas as pl
from jax.experimental.pallas import tpu as pltpu
from jax.sharding import PartitionSpec as P

H = 16
ARRAYS = 5
CONTRACT = (((1,), (1,)), ((), ()))


def attend(groups, meta_ref, *refs):
    blocks, out_ref = refs[:groups], refs[groups]
    runs, _, run_rows, head_size = blocks[0].shape
    rows = runs * run_rows
    patches = meta_ref.shape[0]
    base = head_size ** (-0.5) * math.log2(math.e)

    def flat(ref, which):
        return ref[:, which].reshape(rows, head_size)

    own_group = meta_ref[patches - 1]
    query_at = lax.broadcasted_iota(jnp.int32, (rows, 1), 0) * groups + own_group
    bound = jnp.full((rows, 1), rows * groups, jnp.int32)
    for p in reversed(range(patches - 1)):
        bound = jnp.where(query_at < meta_ref[p], meta_ref[p], bound)

    queries = flat(blocks[0], 0)
    top = total = acc = None
    for offset in range(groups):
        ref = blocks[offset]
        first = 1 if offset == 0 else 0
        source = lax.rem(own_group - offset + groups, groups)
        key_at = lax.broadcasted_iota(jnp.int32, (1, rows), 1) * groups + source
        is_fresh = key_at < bound
        fresh = lax.dot_general(
            queries, flat(ref, first), CONTRACT, preferred_element_type=jnp.float32
        )
        stale = lax.dot_general(
            queries, flat(ref, first + 2), CONTRACT, preferred_element_type=jnp.float32
        )
        scores = jnp.where(is_fresh, fresh, stale)
        block_top = jnp.max(scores, axis=1, keepdims=True)
        new_top = block_top if top is None else jnp.maximum(top, block_top)
        weights = jnp.exp2((scores - new_top) * base)
        block_total = jnp.sum(weights, axis=1, keepdims=True)
        zeroes = jnp.zeros_like(weights)
        part = jnp.dot(
            jnp.where(is_fresh, weights, zeroes).astype(jnp.bfloat16),
            flat(ref, first + 1),
            preferred_element_type=jnp.float32,
        ) + jnp.dot(
            jnp.where(is_fresh, zeroes, weights).astype(jnp.bfloat16),
            flat(ref, first + 3),
            preferred_element_type=jnp.float32,
        )
        if top is None:
            total, acc = block_total, part
        else:
            rescale = jnp.exp2((top - new_top) * base)
            total = total * rescale + block_total
            acc = acc * rescale + part
        top = new_top
    out_ref[...] = (acc / total).astype(out_ref.dtype).reshape(out_ref.shape)


def shards(queries, fresh_keys, fresh_values, stale_keys, stale_values, patch_sizes):
    local_rows, columns = queries.shape
    head_size = columns // H
    devices = lax.axis_size("seq")
    groups = devices // H
    sub_rows = local_rows // groups
    packed = jnp.stack(
        [
            x.reshape(sub_rows, devices, head_size).transpose(1, 0, 2)
            for x in (queries, fresh_keys, fresh_values, stale_keys, stale_values)
        ],
        axis=1,
    )
    moved = lax.all_to_all(packed, "seq", split_axis=0, concat_axis=0, tiled=True)
    if sub_rows % 16:
        moved = moved.transpose(1, 0, 2, 3).reshape(1, ARRAYS, devices * sub_rows, head_size)
    own_group = lax.axis_index("seq") // H
    meta = jnp.concatenate([jnp.cumsum(patch_sizes)[:-1], own_group[None]]).astype(jnp.int32)
    blocks = [moved]
    travelling = moved[:, 1:]
    for _ in range(1, groups):
        route = [((i - H) % devices, i) for i in range(devices)]
        travelling = lax.ppermute(travelling, "seq", route)
        blocks.append(travelling)
    attended = pl.pallas_call(
        functools.partial(attend, groups),
        out_shape=jax.ShapeDtypeStruct(moved.shape[:1] + moved.shape[2:], jnp.bfloat16),
        in_specs=[pl.BlockSpec(memory_space=pltpu.SMEM)]
        + [pl.BlockSpec(memory_space=pltpu.VMEM)] * groups,
        out_specs=pl.BlockSpec(memory_space=pltpu.VMEM),
        compiler_params=pltpu.CompilerParams(vmem_limit_bytes=48 * 1024 * 1024),
        name="attend",
    )(meta, *blocks)
    returned = lax.all_to_all(
        attended.reshape(devices, sub_rows, head_size),
        "seq",
        split_axis=0,
        concat_axis=0,
        tiled=True,
    )
    return returned.transpose(1, 0, 2).reshape(local_rows, columns)


def solution(mesh):
    spec = P(("groups", "seq"), None)
    in_specs = (spec, spec, spec, spec, spec, P("groups"))
    return jax.shard_map(shards, mesh=mesh, in_specs=in_specs, out_specs=spec, check_vma=False)
```

time: 74.9 us -> 44.4 us (0.59)
  waiting for transfers between devices: 33.9 us -> 15.6 us
  starting transfers between devices: 21.6 us -> 7.41 us
  blocking collectives: 10.5 us -> 12.4 us
  Pallas kernels: 0 us -> 1.9 us
  matrix products: 1.53 us -> 0 us
    all_to_all x5 -> x1, waiting for transfers between devices: 33.9 us -> 15.6 us  [shards(): lax.all_to_all(packed, 'seq', split_axis=0, concat_axis=0, tiled=True)]
    all_to_all x5 -> x1, starting transfers between devices: 21.6 us -> 7.41 us  [shards(): lax.all_to_all(packed, 'seq', split_axis=0, concat_axis=0, tiled=True)]
    reshape x5 -> x1, local copies, waits for them, and re-layouts: 3.36 us -> 0.66 us  [shards(): return returned.transpose(1, 0, 2).reshape(local_rows, columns)]
    unnamed x13 -> x16, local copies, waits for them, and re-layouts: 2.66 us -> 5.1 us
    pallas_call x0 -> x1, Pallas kernels: none -> 1.9 us  [shards(): pl.pallas_call(functools.partial(attend, groups), out_shape=jax.ShapeDtyp...]
    all_to_all x1, blocking collectives: 10.5 us -> 12.4 us  [shards(): lax.all_to_all(attended.reshape(devices, sub_rows, head_size), 'seq', spl...]
    dot_general x4 -> x0, matrix products: 1.53 us -> none  [the longest x1 0.47 us: absorb(): jnp.dot(jnp.where(is_fresh, zeroes, rounded), key_block[3], preferred_ele...]
  transfers between devices with their start and end apart: 5 -> 1, of which waited for: 5 -> 1; matrix products, arithmetic and copies ran while one was open for 6% -> 1% of each run, Pallas kernels for 0% -> 0%
where the time goes in v1:
time: 44.4 us; the launch traced here: 44.1 us
  waiting for transfers between devices  15.6 us (35%)
  blocking collectives  12.4 us (28%)
  starting transfers between devices  7.41 us (17%)
  local copies, waits for them, and re-layouts  6.45 us (15%)
  Pallas kernels  1.9 us (4%)
    all_to_all x1, waiting for transfers between devices, shards(): lax.all_to_all(packed, 'seq', split_axis=0, concat_axis=0, tiled=True)  15.6 us
    all_to_all x1, blocking collectives, shards(): lax.all_to_all(attended.reshape(devices, sub_rows, head_size), 'seq', spl...  12.4 us
    all_to_all x1, starting transfers between devices, shards(): lax.all_to_all(packed, 'seq', split_axis=0, concat_axis=0, tiled=True)  7.41 us
    unnamed x16, local copies, waits for them, and re-layouts  5.1 us
    pallas_call x1, Pallas kernels, shards(): pl.pallas_call(functools.partial(attend, groups), out_shape=jax.ShapeDtyp...  1.9 us
  transfers between devices with their start and end apart: 1, of which 1 were waited for; matrix products, arithmetic and copies ran while one was open for 1% of the time, Pallas kernels for 0%

profile of v1, /device:TPU:0, one launch (start us, length us, event | category | flops | bytes accessed | tf_op | source)
XLA Modules:
  0.0 44.1 jit_solution(8764888897338056846)
XLA Ops:
  0.0 0.0 copy-start
  0.0 0.0 copy-start.1
  0.0 0.9 %copy-done = bf16[32,2048]{1,0:T(8,128)(2,1)S(1)} copy-done((bf16[32,2048]{1,0:T(8,128)(2,1)S(1)}, bf16[32,2048]{1,0:T(8,128)(2,1)}, u32[]{:S(2)}) %copy-start) | copy-done | bytes 131096
  0.9 0.7 %fusion.4 = bf16[16,5,32,128]{3,2,1,0:T(8,128)(2,1)} fusion(bf16[32,2048]{1,0:T(8,128)(2,1)S(1)} %copy-done), kind=kLoop, calls=%fused_computation.10 | loop fusion | bytes 262144
  1.6 0.0 copy-done.1
  1.6 0.0 copy-start.2
  1.6 0.7 %fusion.3 = bf16[16,5,32,128]{3,2,1,0:T(8,128)(2,1)} fusion(bf16[16,5,32,128]{3,2,1,0:T(8,128)(2,1)} %fusion.4, bf16[32,2048]{1,0:T(8,128)(2,1)S(1)} %copy-done.1), kind=kLoop, calls=%fused_computation.8 | loop fusion | bytes 262144
  2.3 0.2 copy-done.2
  2.6 0.0 copy-start.3
  2.6 0.7 %fusion.2 = bf16[16,5,32,128]{3,2,1,0:T(8,128)(2,1)} fusion(bf16[16,5,32,128]{3,2,1,0:T(8,128)(2,1)} %fusion.3, bf16[32,2048]{1,0:T(8,128)(2,1)S(1)} %copy-done.2), kind=kLoop, calls=%fused_computation.6 | loop fusion | bytes 262144
  3.3 0.2 copy-done.3
  3.5 0.0 copy-start.4
  3.5 0.7 %fusion.1 = bf16[16,5,32,128]{3,2,1,0:T(8,128)(2,1)} fusion(bf16[16,5,32,128]{3,2,1,0:T(8,128)(2,1)} %fusion.2, bf16[32,2048]{1,0:T(8,128)(2,1)S(1)} %copy-done.3), kind=kLoop, calls=%fused_computation.4 | loop fusion | bytes 262144
  4.2 0.3 copy-done.4
  4.5 0.7 %fusion = bf16[16,5,32,128]{3,2,1,0:T(8,128)(2,1)} fusion(bf16[16,5,32,128]{3,2,1,0:T(8,128)(2,1)} %fusion.1, bf16[32,2048]{1,0:T(8,128)(2,1)S(1)} %copy-done.4), kind=kLoop, calls=%fused_computation.2 | loop fusion | bytes 262144 | tf_op jit(solution)/shard_map/stack | solution.py:77
  5.1 7.4 %all-to-all-start = ((bf16[16,5,32,128]{3,2,1,0:T(8,128)(2,1)}), bf16[16,5,32,128]{3,2,1,0:T(8,128)(2,1)S(1)}, u32[]{:S(2)}, u32[]{:S(2)}) async-start(bf16[16,5,32,128]{3,2,1,0:T(8,128)(2,1)} %fusion), calls=%async_computation | async-start | bytes 1310720 | tf_op jit(solution)/shard_map/all_to_all | solution.py:84
  12.6 0.0 copy-start.5
  12.6 0.6 %copy-done.5 = s32[4]{0:T(128)S(1)} copy-done((s32[4]{0:T(128)S(1)}, s32[4]{0:T(128)}, u32[]{:S(2)}) %copy-start.5) | copy-done | bytes 40
  13.2 0.2 reduce-window.4
  13.4 0.1 pad_add_fusion.meta_ref
  13.5 15.6 %all-to-all-done.refs_0_ = bf16[16,5,32,128]{3,2,1,0:T(8,128)(2,1)S(1)} async-done(((bf16[16,5,32,128]{3,2,1,0:T(8,128)(2,1)}), bf16[16,5,32,128]{3,2,1,0:T(8,128)(2,1)S(1)}, u32[]{:S(2)}, u32[]{:S(2)}) %all-to-all-start) | async-done | bytes 655392 | tf_op jit(solution)/shard_map/all_to_all | solution.py:84
  29.1 1.9 %attend.1 = bf16[16,32,128]{2,1,0:T(8,128)(2,1)S(1)} custom-call(s32[4]{0:T(128)S(1)} %pad_add_fusion.meta_ref, bf16[16,5,32,128]{3,2,1,0:T(8,128)(2,1)S(1)} %all-to-all-done.refs_0_), custom_call_target="tpu_custom_call" | custom-call | tf_op jit(solution)/shard_map/attend/pallas_call | solution.py:95
  31.0 12.4 %all_to_all.10 = bf16[16,32,128]{2,1,0:T(8,128)(2,1)S(1)} all-to-all(bf16[16,32,128]{2,1,0:T(8,128)(2,1)S(1)} %attend.1), channel_id=1, replica_groups=mesh['groups'=2,'seq'=16] {'seq'}, dimensions={0} | all-to-all | bytes 262144 | tf_op jit(solution)/shard_map/all_to_all | solution.py:104
  43.4 0.7 %copy_bitcast_fusion = bf16[32,2048]{1,0:T(8,128)(2,1)} fusion(bf16[16,32,128]{2,1,0:T(8,128)(2,1)S(1)} %all_to_all.10), kind=kLoop, calls=%fused_computation | loop fusion | bytes 262144 | tf_op jit(solution)/shard_map/reshape | solution.py:111
  (1 shorter events, 0.0 us)
Async XLA Ops:
  0.0 0.9 %copy-start = (bf16[32,2048]{1,0:T(8,128)(2,1)S(1)}, bf16[32,2048]{1,0:T(8,128)(2,1)}, u32[]{:S(2)}) copy-start(bf16[32,2048]{1,0:T(8,128)(2,1)} %param.6) | copy-start | bytes 393220
  0.0 1.6 %copy-start.1 = (bf16[32,2048]{1,0:T(8,128)(2,1)S(1)}, bf16[32,2048]{1,0:T(8,128)(2,1)}, u32[]{:S(2)}) copy-start(bf16[32,2048]{1,0:T(8,128)(2,1)} %param.7) | copy-start | bytes 393220
  1.6 1.0 %copy-start.2 = (bf16[32,2048]{1,0:T(8,128)(2,1)S(1)}, bf16[32,2048]{1,0:T(8,128)(2,1)}, u32[]{:S(2)}) copy-start(bf16[32,2048]{1,0:T(8,128)(2,1)} %param.8) | copy-start | bytes 393220
  2.6 1.0 %copy-start.3 = (bf16[32,2048]{1,0:T(8,128)(2,1)S(1)}, bf16[32,2048]{1,0:T(8,128)(2,1)}, u32[]{:S(2)}) copy-start(bf16[32,2048]{1,0:T(8,128)(2,1)} %param.9) | copy-start | bytes 393220
  3.5 1.0 %copy-start.4 = (bf16[32,2048]{1,0:T(8,128)(2,1)S(1)}, bf16[32,2048]{1,0:T(8,128)(2,1)}, u32[]{:S(2)}) copy-start(bf16[32,2048]{1,0:T(8,128)(2,1)} %param.10) | copy-start | bytes 393220
  5.1 24.0 %all-to-all-start = ((bf16[16,5,32,128]{3,2,1,0:T(8,128)(2,1)}), bf16[16,5,32,128]{3,2,1,0:T(8,128)(2,1)S(1)}, u32[]{:S(2)}, u32[]{:S(2)}) async-start(bf16[16,5,32,128]{3,2,1,0:T(8,128)(2,1)} %fusion), calls=%async_computation | async-start | bytes 1310720 | tf_op jit(solution)/shard_map/all_to_all | solution.py:84
  12.6 0.7 %copy-start.5 = (s32[4]{0:T(128)S(1)}, s32[4]{0:T(128)}, u32[]{:S(2)}) copy-start(s32[4]{0:T(128)} %param.11) | copy-start | bytes 52

commit v2 on v1

--- a/solution.py
+++ b/solution.py
@@ -13,21 +13,23 @@
 CONTRACT = (((1,), (1,)), ((), ()))
 
 
-def attend(groups, meta_ref, *refs):
+def attend(groups, sizes_ref, *refs):
     blocks, out_ref = refs[:groups], refs[groups]
     runs, _, run_rows, head_size = blocks[0].shape
     rows = runs * run_rows
-    patches = meta_ref.shape[0]
+    ends = [sizes_ref[0]]
+    for p in range(1, sizes_ref.shape[0] - 1):
+        ends.append(ends[-1] + sizes_ref[p])
     base = head_size ** (-0.5) * math.log2(math.e)
 
     def flat(ref, which):
         return ref[:, which].reshape(rows, head_size)
 
-    own_group = meta_ref[patches - 1]
+    own_group = lax.axis_index("seq") // H
     query_at = lax.broadcasted_iota(jnp.int32, (rows, 1), 0) * groups + own_group
     bound = jnp.full((rows, 1), rows * groups, jnp.int32)
-    for p in reversed(range(patches - 1)):
-        bound = jnp.where(query_at < meta_ref[p], meta_ref[p], bound)
+    for end in reversed(ends):
+        bound = jnp.where(query_at < end, end, bound)
 
     queries = flat(blocks[0], 0)
     top = total = acc = None
@@ -68,24 +70,50 @@
     out_ref[...] = (acc / total).astype(out_ref.dtype).reshape(out_ref.shape)
 
 
+def pack(*refs):
+    sources, out_ref, staged, arrived = refs[:ARRAYS], *refs[ARRAYS:]
+    head_size = out_ref.shape[-1]
+    copies = [
+        pltpu.make_async_copy(source, staged.at[a], arrived.at[a])
+        for a, source in enumerate(sources)
+    ]
+    for copy in copies:
+        copy.start()
+    for a, copy in enumerate(copies):
+        copy.wait()
+        for d in range(out_ref.shape[0]):
+            out_ref[d, a] = staged[a, :, d * head_size : (d + 1) * head_size]
+
+
 def shards(queries, fresh_keys, fresh_values, stale_keys, stale_values, patch_sizes):
     local_rows, columns = queries.shape
     head_size = columns // H
     devices = lax.axis_size("seq")
     groups = devices // H
     sub_rows = local_rows // groups
-    packed = jnp.stack(
-        [
-            x.reshape(sub_rows, devices, head_size).transpose(1, 0, 2)
-            for x in (queries, fresh_keys, fresh_values, stale_keys, stale_values)
-        ],
-        axis=1,
-    )
+    arrays = (queries, fresh_keys, fresh_values, stale_keys, stale_values)
+    if groups == 1 and sub_rows % 16 == 0:
+        packed = pl.pallas_call(
+            pack,
+            out_shape=jax.ShapeDtypeStruct(
+                (devices, ARRAYS, sub_rows, head_size), queries.dtype
+            ),
+            in_specs=[pl.BlockSpec(memory_space=pl.ANY)] * ARRAYS,
+            out_specs=pl.BlockSpec(memory_space=pltpu.VMEM),
+            scratch_shapes=[
+                pltpu.VMEM((ARRAYS, local_rows, columns), queries.dtype),
+                pltpu.SemaphoreType.DMA((ARRAYS,)),
+            ],
+            name="pack",
+        )(*arrays)
+    else:
+        packed = jnp.stack(
+            [x.reshape(sub_rows, devices, head_size).transpose(1, 0, 2) for x in arrays],
+            axis=1,
+        )
     moved = lax.all_to_all(packed, "seq", split_axis=0, concat_axis=0, tiled=True)
     if sub_rows % 16:
         moved = moved.transpose(1, 0, 2, 3).reshape(1, ARRAYS, devices * sub_rows, head_size)
-    own_group = lax.axis_index("seq") // H
-    meta = jnp.concatenate([jnp.cumsum(patch_sizes)[:-1], own_group[None]]).astype(jnp.int32)
     blocks = [moved]
     travelling = moved[:, 1:]
     for _ in range(1, groups):
@@ -100,7 +128,7 @@
         out_specs=pl.BlockSpec(memory_space=pltpu.VMEM),
         compiler_params=pltpu.CompilerParams(vmem_limit_bytes=48 * 1024 * 1024),
         name="attend",
-    )(meta, *blocks)
+    )(patch_sizes, *blocks)
     returned = lax.all_to_all(
         attended.reshape(devices, sub_rows, head_size),
         "seq",

time: 44.4 us -> 41.5 us (0.935)
  blocking collectives: 12.4 us -> 36.6 us
  waiting for transfers between devices: 15.6 us -> 0 us
  starting transfers between devices: 7.41 us -> 0 us
  local copies, waits for them, and re-layouts: 6.45 us -> 0.67 us
  Pallas kernels: 1.9 us -> 3.97 us
    all_to_all x0 -> x1, blocking collectives: none -> 25.7 us  [shards(): lax.all_to_all(packed, 'seq', split_axis=0, concat_axis=0, tiled=True)]
    all_to_all x1 -> x0, waiting for transfers between devices: 15.6 us -> none  [shards(): lax.all_to_all(packed, 'seq', split_axis=0, concat_axis=0, tiled=True)]
    all_to_all x1 -> x0, starting transfers between devices: 7.41 us -> none  [shards(): lax.all_to_all(packed, 'seq', split_axis=0, concat_axis=0, tiled=True)]
    unnamed x16 -> x2, local copies, waits for them, and re-layouts: 5.1 us -> 0.01 us
    pallas_call x0 -> x1, Pallas kernels: none -> 2.07 us  [shards(): pl.pallas_call(pack, out_shape=jax.ShapeDtypeStruct((devices, ARRAYS, sub...]
    all_to_all x1, blocking collectives: 12.4 us -> 10.9 us  [shards(): lax.all_to_all(attended.reshape(devices, sub_rows, head_size), 'seq', spl...]
    another operation x1 -> x0, local copies, waits for them, and re-layouts: 0.68 us -> none  [shards(): jnp.stack([x.reshape(sub_rows, devices, head_size).transpose(1, 0, 2) for...]
  transfers between devices with their start and end apart: 1 -> 0, of which waited for: 1 -> 0; matrix products, arithmetic and copies ran while one was open for 1% -> 0% of each run, Pallas kernels for 0% -> 0%
where the time goes in v2:
time: 41.5 us; the launch traced here: 41.3 us
  blocking collectives  36.6 us (88%)
  Pallas kernels  3.97 us (10%)
  local copies, waits for them, and re-layouts  0.67 us (2%)
    all_to_all x1, blocking collectives, shards(): lax.all_to_all(packed, 'seq', split_axis=0, concat_axis=0, tiled=True)  25.7 us
    all_to_all x1, blocking collectives, shards(): lax.all_to_all(attended.reshape(devices, sub_rows, head_size), 'seq', spl...  10.9 us
    pallas_call x1, Pallas kernels, shards(): pl.pallas_call(pack, out_shape=jax.ShapeDtypeStruct((devices, ARRAYS, sub...  2.07 us
    pallas_call x1, Pallas kernels, shards(): pl.pallas_call(functools.partial(attend, groups), out_shape=jax.ShapeDtyp...  1.9 us

profile of v2, /device:TPU:0, one launch (start us, length us, event | category | flops | bytes accessed | tf_op | source)
XLA Modules:
  0.0 41.3 jit_solution(3927951908210998278)
XLA Ops:
  0.0 2.1 %pack.1 = bf16[16,5,32,128]{3,2,1,0:T(8,128)(2,1)} custom-call(bf16[32,2048]{1,0:T(8,128)(2,1)} %refs_0_.1, bf16[32,2048]{1,0:T(8,128)(2,1)} %refs_1_.1, bf16[32,2048]{1,0:T(8,128)(2,1)} %refs_2_.1, bf16[32,2048]{1,0:T(8,128)(2,1)} %refs_3_.1, bf16[32,2048]{1,0:T(8,128)(2,1)} %refs_4_.1), custom_call_target="tpu_custom_call" | custom-call | tf_op jit(solution)/shard_map/pack/pallas_call | solution.py:96
  2.1 0.0 copy-start
  2.1 25.7 %all_to_all.10.refs_0_ = bf16[16,5,32,128]{3,2,1,0:T(8,128)(2,1)S(1)} all-to-all(bf16[16,5,32,128]{3,2,1,0:T(8,128)(2,1)} %pack.1), channel_id=1, replica_groups=mesh['groups'=2,'seq'=16] {'seq'}, dimensions={0} | all-to-all | bytes 1310720 | tf_op jit(solution)/shard_map/all_to_all | solution.py:114
  27.8 0.0 copy-done
  27.8 1.9 %attend.1 = bf16[16,32,128]{2,1,0:T(8,128)(2,1)S(1)} custom-call(s32[4]{0:T(128)S(1)} %copy-done, bf16[16,5,32,128]{3,2,1,0:T(8,128)(2,1)S(1)} %all_to_all.10.refs_0_), custom_call_target="tpu_custom_call" | custom-call | tf_op jit(solution)/shard_map/attend/pallas_call | solution.py:123
  29.7 10.9 %all_to_all.11 = bf16[16,32,128]{2,1,0:T(8,128)(2,1)S(1)} all-to-all(bf16[16,32,128]{2,1,0:T(8,128)(2,1)S(1)} %attend.1), channel_id=1, replica_groups=mesh['groups'=2,'seq'=16] {'seq'}, dimensions={0} | all-to-all | bytes 262144 | tf_op jit(solution)/shard_map/all_to_all | solution.py:132
  40.6 0.7 %copy_bitcast_fusion = bf16[32,2048]{1,0:T(8,128)(2,1)} fusion(bf16[16,32,128]{2,1,0:T(8,128)(2,1)S(1)} %all_to_all.11), kind=kLoop, calls=%fused_computation | loop fusion | bytes 262144 | tf_op jit(solution)/shard_map/reshape | solution.py:139
Async XLA Ops:
  2.1 25.7 %copy-start = (s32[4]{0:T(128)S(1)}, s32[4]{0:T(128)}, u32[]{:S(2)}) copy-start(s32[4]{0:T(128)} %sizes_ref.1) | copy-start | bytes 52

commit v3 on v2

--- a/solution.py
+++ b/solution.py
@@ -10,6 +10,7 @@
 
 H = 16
 ARRAYS = 5
+CHUNKS = 2
 CONTRACT = (((1,), (1,)), ((), ()))
 
 
@@ -31,43 +32,52 @@
     for end in reversed(ends):
         bound = jnp.where(query_at < end, end, bound)
 
-    queries = flat(blocks[0], 0)
-    top = total = acc = None
-    for offset in range(groups):
-        ref = blocks[offset]
-        first = 1 if offset == 0 else 0
-        source = lax.rem(own_group - offset + groups, groups)
-        key_at = lax.broadcasted_iota(jnp.int32, (1, rows), 1) * groups + source
-        is_fresh = key_at < bound
-        fresh = lax.dot_general(
-            queries, flat(ref, first), CONTRACT, preferred_element_type=jnp.float32
-        )
-        stale = lax.dot_general(
-            queries, flat(ref, first + 2), CONTRACT, preferred_element_type=jnp.float32
-        )
-        scores = jnp.where(is_fresh, fresh, stale)
-        block_top = jnp.max(scores, axis=1, keepdims=True)
-        new_top = block_top if top is None else jnp.maximum(top, block_top)
-        weights = jnp.exp2((scores - new_top) * base)
-        block_total = jnp.sum(weights, axis=1, keepdims=True)
-        zeroes = jnp.zeros_like(weights)
-        part = jnp.dot(
-            jnp.where(is_fresh, weights, zeroes).astype(jnp.bfloat16),
-            flat(ref, first + 1),
-            preferred_element_type=jnp.float32,
-        ) + jnp.dot(
-            jnp.where(is_fresh, zeroes, weights).astype(jnp.bfloat16),
-            flat(ref, first + 3),
-            preferred_element_type=jnp.float32,
-        )
-        if top is None:
-            total, acc = block_total, part
+    chunk = rows // CHUNKS
+    for at in range(0, rows, chunk):
+        queries = flat(blocks[0], 0)[at : at + chunk]
+        edge = bound[at : at + chunk]
+        top = total = acc = None
+        for offset in range(groups):
+            ref = blocks[offset]
+            first = 1 if offset == 0 else 0
+            source = lax.rem(own_group - offset + groups, groups)
+            key_at = lax.broadcasted_iota(jnp.int32, (1, rows), 1) * groups + source
+            is_fresh = key_at < edge
+            fresh = lax.dot_general(
+                queries, flat(ref, first), CONTRACT, preferred_element_type=jnp.float32
+            )
+            stale = lax.dot_general(
+                queries, flat(ref, first + 2), CONTRACT, preferred_element_type=jnp.float32
+            )
+            scores = jnp.where(is_fresh, fresh, stale)
+            block_top = jnp.max(scores, axis=1, keepdims=True)
+            new_top = block_top if top is None else jnp.maximum(top, block_top)
+            weights = jnp.exp2((scores - new_top) * base)
+            block_total = jnp.sum(weights, axis=1, keepdims=True)
+            zeroes = jnp.zeros_like(weights)
+            part = jnp.dot(
+                jnp.where(is_fresh, weights, zeroes).astype(jnp.bfloat16),
+                flat(ref, first + 1),
+                preferred_element_type=jnp.float32,
+            ) + jnp.dot(
+                jnp.where(is_fresh, zeroes, weights).astype(jnp.bfloat16),
+                flat(ref, first + 3),
+                preferred_element_type=jnp.float32,
+            )
+            if top is None:
+                total, acc = block_total, part
+            else:
+                rescale = jnp.exp2((top - new_top) * base)
+                total = total * rescale + block_total
+                acc = acc * rescale + part
+            top = new_top
+        done = (acc / total).astype(out_ref.dtype)
+        if run_rows == rows:
+            out_ref[0, at : at + chunk] = done
         else:
-            rescale = jnp.exp2((top - new_top) * base)
-            total = total * rescale + block_total
-            acc = acc * rescale + part
-        top = new_top
-    out_ref[...] = (acc / total).astype(out_ref.dtype).reshape(out_ref.shape)
+            out_ref[at // run_rows : (at + chunk) // run_rows] = done.reshape(
+                chunk // run_rows, run_rows, head_size
+            )
 
 
 def pack(*refs):
@@ -95,9 +105,7 @@
     if groups == 1 and sub_rows % 16 == 0:
         packed = pl.pallas_call(
             pack,
-            out_shape=jax.ShapeDtypeStruct(
-                (devices, ARRAYS, sub_rows, head_size), queries.dtype
-            ),
+            out_shape=pltpu.VMEM((devices, ARRAYS, sub_rows, head_size), queries.dtype),
             in_specs=[pl.BlockSpec(memory_space=pl.ANY)] * ARRAYS,
             out_specs=pl.BlockSpec(memory_space=pltpu.VMEM),
             scratch_shapes=[

time: 41.5 us -> 40.2 us (0.969)
  Pallas kernels: 3.97 us -> 2.91 us
    pallas_call x1, Pallas kernels: 2.07 us -> 1.23 us  [shards(): pl.pallas_call(pack, out_shape=pltpu.VMEM((devices, ARRAYS, sub_rows, hea...]
where the time goes in v3:
time: 40.2 us; the launch traced here: 40 us
  blocking collectives  36.4 us (91%)
  Pallas kernels  2.91 us (7%)
  local copies, waits for them, and re-layouts  0.67 us (2%)
    all_to_all x1, blocking collectives, shards(): lax.all_to_all(packed, 'seq', split_axis=0, concat_axis=0, tiled=True)  25.5 us
    all_to_all x1, blocking collectives, shards(): lax.all_to_all(attended.reshape(devices, sub_rows, head_size), 'seq', spl...  10.9 us
    pallas_call x1, Pallas kernels, shards(): pl.pallas_call(functools.partial(attend, groups), out_shape=jax.ShapeDtyp...  1.68 us
    pallas_call x1, Pallas kernels, shards(): pl.pallas_call(pack, out_shape=pltpu.VMEM((devices, ARRAYS, sub_rows, hea...  1.23 us

profile of v3, /device:TPU:0, one launch (start us, length us, event | category | flops | bytes accessed | tf_op | source)
XLA Modules:
  0.0 40.0 jit_solution(12992669088546485747)
XLA Ops:
  0.0 1.2 %pack.1 = bf16[16,5,32,128]{3,2,1,0:T(8,128)(2,1)S(1)} custom-call(bf16[32,2048]{1,0:T(8,128)(2,1)} %refs_0_.1, bf16[32,2048]{1,0:T(8,128)(2,1)} %refs_1_.1, bf16[32,2048]{1,0:T(8,128)(2,1)} %refs_2_.1, bf16[32,2048]{1,0:T(8,128)(2,1)} %refs_3_.1, bf16[32,2048]{1,0:T(8,128)(2,1)} %refs_4_.1), custom_call_target="tpu_custom_call" | custom-call | tf_op jit(solution)/shard_map/pack/pallas_call | solution.py:106
  1.2 0.0 copy-start
  1.2 25.5 %all_to_all.10.refs_0_ = bf16[16,5,32,128]{3,2,1,0:T(8,128)(2,1)S(1)} all-to-all(bf16[16,5,32,128]{3,2,1,0:T(8,128)(2,1)S(1)} %pack.1), channel_id=1, replica_groups=mesh['groups'=2,'seq'=16] {'seq'}, dimensions={0} | all-to-all | bytes 1310720 | tf_op jit(solution)/shard_map/all_to_all | solution.py:122
  26.7 0.0 copy-done
  26.7 1.7 %attend.1 = bf16[16,32,128]{2,1,0:T(8,128)(2,1)S(1)} custom-call(s32[4]{0:T(128)S(1)} %copy-done, bf16[16,5,32,128]{3,2,1,0:T(8,128)(2,1)S(1)} %all_to_all.10.refs_0_), custom_call_target="tpu_custom_call" | custom-call | tf_op jit(solution)/shard_map/attend/pallas_call | solution.py:131
  28.4 10.9 %all_to_all.11 = bf16[16,32,128]{2,1,0:T(8,128)(2,1)S(1)} all-to-all(bf16[16,32,128]{2,1,0:T(8,128)(2,1)S(1)} %attend.1), channel_id=1, replica_groups=mesh['groups'=2,'seq'=16] {'seq'}, dimensions={0} | all-to-all | bytes 262144 | tf_op jit(solution)/shard_map/all_to_all | solution.py:140
  39.3 0.7 %copy_bitcast_fusion = bf16[32,2048]{1,0:T(8,128)(2,1)} fusion(bf16[16,32,128]{2,1,0:T(8,128)(2,1)S(1)} %all_to_all.11), kind=kLoop, calls=%fused_computation | loop fusion | bytes 262144 | tf_op jit(solution)/shard_map/reshape | solution.py:147
Async XLA Ops:
  1.2 25.5 %copy-start = (s32[4]{0:T(128)S(1)}, s32[4]{0:T(128)}, u32[]{:S(2)}) copy-start(s32[4]{0:T(128)} %sizes_ref.1) | copy-start | bytes 52

commit v4 on v3

--- a/solution.py
+++ b/solution.py
@@ -10,7 +10,7 @@
 
 H = 16
 ARRAYS = 5
-CHUNKS = 2
+CHUNKS = 1
 CONTRACT = (((1,), (1,)), ((), ()))
 
 
@@ -27,41 +27,41 @@
         return ref[:, which].reshape(rows, head_size)
 
     own_group = lax.axis_index("seq") // H
-    query_at = lax.broadcasted_iota(jnp.int32, (rows, 1), 0) * groups + own_group
-    bound = jnp.full((rows, 1), rows * groups, jnp.int32)
+    query_at = lax.broadcasted_iota(jnp.int32, (1, rows), 1) * groups + own_group
+    bound = jnp.full((1, rows), rows * groups, jnp.int32)
     for end in reversed(ends):
         bound = jnp.where(query_at < end, end, bound)
 
     chunk = rows // CHUNKS
     for at in range(0, rows, chunk):
         queries = flat(blocks[0], 0)[at : at + chunk]
-        edge = bound[at : at + chunk]
+        edge = bound[:, at : at + chunk]
         top = total = acc = None
         for offset in range(groups):
             ref = blocks[offset]
             first = 1 if offset == 0 else 0
             source = lax.rem(own_group - offset + groups, groups)
-            key_at = lax.broadcasted_iota(jnp.int32, (1, rows), 1) * groups + source
+            key_at = lax.broadcasted_iota(jnp.int32, (rows, 1), 0) * groups + source
             is_fresh = key_at < edge
             fresh = lax.dot_general(
-                queries, flat(ref, first), CONTRACT, preferred_element_type=jnp.float32
+                flat(ref, first), queries, CONTRACT, preferred_element_type=jnp.float32
             )
             stale = lax.dot_general(
-                queries, flat(ref, first + 2), CONTRACT, preferred_element_type=jnp.float32
+                flat(ref, first + 2), queries, CONTRACT, preferred_element_type=jnp.float32
             )
             scores = jnp.where(is_fresh, fresh, stale)
-            block_top = jnp.max(scores, axis=1, keepdims=True)
+            block_top = jnp.max(scores, axis=0, keepdims=True)
             new_top = block_top if top is None else jnp.maximum(top, block_top)
             weights = jnp.exp2((scores - new_top) * base)
-            block_total = jnp.sum(weights, axis=1, keepdims=True)
+            block_total = jnp.sum(weights, axis=0, keepdims=True)
             zeroes = jnp.zeros_like(weights)
             part = jnp.dot(
+                flat(ref, first + 1).T,
                 jnp.where(is_fresh, weights, zeroes).astype(jnp.bfloat16),
-                flat(ref, first + 1),
                 preferred_element_type=jnp.float32,
             ) + jnp.dot(
+                flat(ref, first + 3).T,
                 jnp.where(is_fresh, zeroes, weights).astype(jnp.bfloat16),
-                flat(ref, first + 3),
                 preferred_element_type=jnp.float32,
             )
             if top is None:
@@ -71,7 +71,7 @@
                 total = total * rescale + block_total
                 acc = acc * rescale + part
             top = new_top
-        done = (acc / total).astype(out_ref.dtype)
+        done = (acc / total).T.astype(out_ref.dtype)
         if run_rows == rows:
             out_ref[0, at : at + chunk] = done
         else:

time: 40.2 us -> 40.1 us (level)
  no operation moved by 1% of the time
where the time goes in v4:
time: 40.1 us; the launch traced here: 39.9 us
  blocking collectives  36.4 us (91%)
  Pallas kernels  2.88 us (7%)
  local copies, waits for them, and re-layouts  0.67 us (2%)
    all_to_all x1, blocking collectives, shards(): lax.all_to_all(packed, 'seq', split_axis=0, concat_axis=0, tiled=True)  25.5 us
    all_to_all x1, blocking collectives, shards(): lax.all_to_all(attended.reshape(devices, sub_rows, head_size), 'seq', spl...  10.9 us
    pallas_call x1, Pallas kernels, shards(): pl.pallas_call(functools.partial(attend, groups), out_shape=jax.ShapeDtyp...  1.65 us
    pallas_call x1, Pallas kernels, shards(): pl.pallas_call(pack, out_shape=pltpu.VMEM((devices, ARRAYS, sub_rows, hea...  1.23 us

profile of v4, /device:TPU:0, one launch (start us, length us, event | category | flops | bytes accessed | tf_op | source)
XLA Modules:
  0.0 39.9 jit_solution(9989872483180900803)
XLA Ops:
  0.0 1.2 %pack.1 = bf16[16,5,32,128]{3,2,1,0:T(8,128)(2,1)S(1)} custom-call(bf16[32,2048]{1,0:T(8,128)(2,1)} %refs_0_.1, bf16[32,2048]{1,0:T(8,128)(2,1)} %refs_1_.1, bf16[32,2048]{1,0:T(8,128)(2,1)} %refs_2_.1, bf16[32,2048]{1,0:T(8,128)(2,1)} %refs_3_.1, bf16[32,2048]{1,0:T(8,128)(2,1)} %refs_4_.1), custom_call_target="tpu_custom_call" | custom-call | tf_op jit(solution)/shard_map/pack/pallas_call | solution.py:106
  1.2 0.0 copy-start
  1.2 25.5 %all_to_all.10.refs_0_ = bf16[16,5,32,128]{3,2,1,0:T(8,128)(2,1)S(1)} all-to-all(bf16[16,5,32,128]{3,2,1,0:T(8,128)(2,1)S(1)} %pack.1), channel_id=1, replica_groups=mesh['groups'=2,'seq'=16] {'seq'}, dimensions={0} | all-to-all | bytes 1310720 | tf_op jit(solution)/shard_map/all_to_all | solution.py:122
  26.7 0.0 copy-done
  26.7 1.7 %attend.1 = bf16[16,32,128]{2,1,0:T(8,128)(2,1)S(1)} custom-call(s32[4]{0:T(128)S(1)} %copy-done, bf16[16,5,32,128]{3,2,1,0:T(8,128)(2,1)S(1)} %all_to_all.10.refs_0_), custom_call_target="tpu_custom_call" | custom-call | tf_op jit(solution)/shard_map/attend/pallas_call | solution.py:131
  28.4 10.9 %all_to_all.11 = bf16[16,32,128]{2,1,0:T(8,128)(2,1)S(1)} all-to-all(bf16[16,32,128]{2,1,0:T(8,128)(2,1)S(1)} %attend.1), channel_id=1, replica_groups=mesh['groups'=2,'seq'=16] {'seq'}, dimensions={0} | all-to-all | bytes 262144 | tf_op jit(solution)/shard_map/all_to_all | solution.py:140
  39.3 0.7 %copy_bitcast_fusion = bf16[32,2048]{1,0:T(8,128)(2,1)} fusion(bf16[16,32,128]{2,1,0:T(8,128)(2,1)S(1)} %all_to_all.11), kind=kLoop, calls=%fused_computation | loop fusion | bytes 262144 | tf_op jit(solution)/shard_map/reshape | solution.py:147
Async XLA Ops:
  1.2 25.5 %copy-start = (s32[4]{0:T(128)S(1)}, s32[4]{0:T(128)}, u32[]{:S(2)}) copy-start(s32[4]{0:T(128)} %sizes_ref.1) | copy-start | bytes 52
